TPU v7x, 512 devices: a whole 4x4x16 slice. The times are simulated.
512 devices in a mesh: row: 32 (over z, core), col: 16 (over x, y).
Axes of the slice: x: 4, y: 4, z: 16, core: 2. Of those that a mesh axis runs over, the one named last changes fastest.
Arguments:
- factor: bfloat16 [8192, 8192], P('row', 'col'), as said below
- sel_tiles: int32 [32], replicated, may hold values from 0 to 63, as said below
- coupling: bfloat16 [8192, 2048], P('col', 'row')
Outputs:
- root_inverse: float32 [8192, 8192], P('row', 'col')
- child_inverse: float32 [2048, 8192], P('col', 'row')
Inputs may be any that keep to these rules, and one draw needn't show every extreme that they name: sel_tiles holds 32 distinct tile indices in increasing order; rows of coupling outside the listed tiles are zero. factor is lower triangular with a diagonal between 1 and 1.5.
All inputs are finite; a program needn't handle non-finite values.
Results may differ from a plain program's by a relative error of at most 0.003.
Values may be sent and summed in bfloat16 or wider, within the bound.
A program may use at most 64 MiB of HBM per device.

v0:
```python
import jax
import jax.numpy as jnp
from jax import lax
from jax.sharding import PartitionSpec as P

TILE = 128


def from_root(value, axis, source):
    kept = jnp.where(lax.axis_index(axis) == source, value, 0).astype(value.dtype)
    return lax.psum(kept, axis)


def in_blocks(value, dim, devices):
    lengths = value.shape
    parts = value.reshape(*lengths[:dim], devices, lengths[dim] // devices, *lengths[dim + 1 :])
    return jnp.moveaxis(parts, dim, 0)


def summed_on_arrival(value, axis, dim):
    devices = lax.axis_size(axis)
    parts = lax.all_to_all(in_blocks(value, dim, devices), axis, 0, 0, tiled=True)
    return jnp.sum(parts, axis=0)


def body(factor, sel_tiles, coupling):
    rows_here = factor.shape[0]
    row_index = lax.axis_index("row")
    whole = lax.all_gather(factor, "row", axis=0, tiled=True)
    ratio = lax.axis_size("row") // lax.axis_size("col")
    offset = row_index % ratio * rows_here
    piece = lax.dynamic_slice_in_dim(whole, offset, rows_here, 1)
    partner = from_root(piece, "col", row_index // ratio)
    gram = lax.dot_general(
        partner, whole, (((0,), (0,)), ((), ())), preferred_element_type=jnp.float32
    )
    coupling_full = lax.all_gather(coupling, "row", axis=1, tiled=True)
    rounded = gram.astype(jnp.bfloat16)
    global_rows = row_index * rows_here + jnp.arange(rows_here, dtype=jnp.int32)
    member = jnp.any((global_rows // TILE)[:, None] == sel_tiles[None, :], axis=1)
    summed = summed_on_arrival(
        lax.dot_general(
            coupling_full, rounded, (((0,), (1,)), ((), ())), preferred_element_type=jnp.float32
        ),
        "col",
        0,
    )
    child = jnp.where(member[None, :], -summed, jnp.float32(0.0))
    return (gram, child)


def solution(mesh):
    placed = (P("row", "col"), P(), P("col", "row"))
    return jax.shard_map(
        body,
        mesh=mesh,
        in_specs=placed,
        out_specs=(P("row", "col"), P("col", "row")),
        check_vma=False,
    )
```

profile of v0, /device:TPU:1, one launch (start us, length us, event | category | flops | bytes accessed | tf_op | source)
XLA Modules:
  0.0 351.0 jit_solution(12061191900237767093)
XLA Ops:
  7.2 0.0 all-gather.3.cloned.1.call-start
  7.2 0.7 all-gather.3.cloned.1.call-update
  7.9 0.0 all-reduce.2.cloned.1.call-start
  8.0 86.6 %all-gather.3.cloned.1.call-done = bf16[8192,512]{1,0:T(8,128)(2,1)} async-done(((bf16[256,512]{1,0:T(8,128)(2,1)}), bf16[8192,512]{1,0:T(8,128)(2,1)}) %all-gather.3.cloned.1.call-update) | async-done | bytes 8388624 | tf_op jit(solution)/shard_map/all_gather | solution.py:29
  94.6 4.9 %dynamic-slice_select_fusion = bf16[8192,256]{1,0:T(8,128)(2,1)} fusion(bf16[8192,512]{1,0:T(8,128)(2,1)} %all-gather.3.cloned.1.call-done, s32[]{:T(128)S(6)} %select_n.38, pred[]{:T(512)S(6)} %eq.18), kind=kLoop, calls=%fused_computation | loop fusion | flops 2097152 | bytes 8388613 | tf_op jit(solution)/shard_map/jit(_where)/select_n | solution.py:10
  99.4 0.0 all-reduce.2.cloned.1.call-update
  99.5 0.0 all-gather.5.cloned.1.call-start
  99.5 0.7 all-gather.5.cloned.1.call-update
  100.2 129.5 %all-reduce.2.cloned.1.call-done = bf16[8192,256]{1,0:T(8,128)(2,1)} async-done(((bf16[8192,256]{1,0:T(8,128)(2,1)}), bf16[8192,256]{1,0:T(8,128)(2,1)}) %all-reduce.2.cloned.1.call-update) | async-done | bytes 4194320 | tf_op jit(solution)/shard_map/psum | solution.py:11
  229.7 7.0 %fusion.1 = f32[256,512]{1,0:T(8,128)S(1)} fusion(bf16[8192,256]{1,0:T(8,128)(2,1)} %all-reduce.2.cloned.1.call-done, bf16[8192,512]{1,0:T(8,128)(2,1)} %all-gather.3.cloned.1.call-done), kind=kOutput, calls=%fused_computation.10 | convolution fusion | flops 2147483648 | bytes 13107200 | tf_op jit(solution)/shard_map/dot_general | solution.py:34
  236.7 0.0 copy-start
  236.7 67.2 %all-gather.5.cloned.1.call-done = bf16[512,2048]{0,1:T(8,128)(2,1)} async-done(((bf16[512,64]{0,1:T(8,128)(2,1)}), bf16[512,2048]{0,1:T(8,128)(2,1)}) %all-gather.5.cloned.1.call-update) | async-done | bytes 2097168 | tf_op jit(solution)/shard_map/all_gather | solution.py:37
  303.9 2.3 convolution_bitcast_fusion
  306.2 0.0 copy-start.1
  306.2 1.5 copy.14
  307.8 0.0 copy-done
  307.8 6.5 %all-to-all-start = ((f32[16,128,256]{1,2,0:T(8,128)}), f32[16,128,256]{1,2,0:T(8,128)S(1)}, u32[]{:S(2)}, u32[]{:S(2)}) async-start(f32[16,128,256]{1,2,0:T(8,128)} %bitcast.9), calls=%async_computation | async-start | bytes 4194304 | tf_op jit(solution)/shard_map/all_to_all | solution.py:22
  314.3 0.0 copy-done.1
  314.4 0.1 compare_reduce_fusion
  314.5 29.1 %all-to-all-done = f32[16,128,256]{1,2,0:T(8,128)S(1)} async-done(((f32[16,128,256]{1,2,0:T(8,128)}), f32[16,128,256]{1,2,0:T(8,128)S(1)}, u32[]{:S(2)}, u32[]{:S(2)}) %all-to-all-start) | async-done | bytes 2097184 | tf_op jit(solution)/shard_map/all_to_all | solution.py:22
  343.5 0.1 reduce_sum.9
  343.6 0.1 negate_select_fusion
  343.7 0.8 copy.10
  (1 shorter events, 0.0 us)
Async XLA Ops:
  7.2 87.4 %all-gather.3.cloned.1.call-start = ((), (), s32[]{:S(2)}) async-start(), calls=%async_computation.1 | async-start | bytes 8650752 | tf_op jit(solution)/shard_map/all_gather | solution.py:29
  7.9 221.8 %all-reduce.2.cloned.1.call-start = ((), (), s32[]{:S(2)}) async-start(), calls=%async_computation.2 | async-start | bytes 8388608 | tf_op jit(solution)/shard_map/psum | solution.py:11
  99.5 204.4 %all-gather.5.cloned.1.call-start = ((), (), s32[]{:S(2)}) async-start(), calls=%async_computation.3 | async-start | bytes 2162688 | tf_op jit(solution)/shard_map/all_gather | solution.py:37
  236.7 71.1 %copy-start = (f32[256,512]{1,0:T(8,128)}, f32[256,512]{1,0:T(8,128)S(1)}, u32[]{:S(2)}) copy-start(f32[256,512]{1,0:T(8,128)S(1)} %fusion.1) | copy-start | bytes 1572868
  306.2 8.1 %copy-start.1 = (s32[32]{0:T(128)S(1)}, s32[32]{0:T(128)}, u32[]{:S(2)}) copy-start(s32[32]{0:T(128)} %param.4) | copy-start | bytes 388
  307.8 35.7 %all-to-all-start = ((f32[16,128,256]{1,2,0:T(8,128)}), f32[16,128,256]{1,2,0:T(8,128)S(1)}, u32[]{:S(2)}, u32[]{:S(2)}) async-start(f32[16,128,256]{1,2,0:T(8,128)} %bitcast.9), calls=%async_computation | async-start | bytes 4194304 | tf_op jit(solution)/shard_map/all_to_all | solution.py:22
Sparse Core Ops, SparseCore 0:
  10.1 84.4 all-gather.2
  99.6 130.0 all-reduce.1
  231.8 72.0 all-gather.4
where the time goes:
time: 352 us; the launch traced here: 351 us
  waiting for transfers between devices  314 us (89%)
  between operations  13.8 us (4%)
  matrix products  9.31 us (3%)
  starting transfers between devices  6.65 us (2%)
  other arithmetic  5.17 us (1%)
    psum x1, waiting for transfers between devices, from_root(): return lax.psum(kept, axis)  130 us
    all_gather x1, waiting for transfers between devices, body(): whole = lax.all_gather(factor, 'row', axis=0, tiled=True)  86.6 us
    all_gather x1, waiting for transfers between devices, body(): coupling_full = lax.all_gather(coupling, 'row', axis=1, tiled=True)  67.2 us
    all_to_all x1, waiting for transfers between devices, summed_on_arrival(): lax.all_to_all(in_blocks(value, dim, devices), axis, 0, 0, tiled=True)  29.1 us
  transfers between devices with their start and end apart: 4, of which 4 were waited for; matrix products, arithmetic and copies ran while one was open for 2% of the time, Pallas kernels for 0%

commit v1 on v0

v1 whole, which is shorter than its diff:
```python
import functools

import jax
import jax.numpy as jnp
from jax import lax
from jax.experimental import pallas as pl
from jax.experimental.pallas import tpu as pltpu
from jax.sharding import PartitionSpec as P

TILE = 128
MESH = pl.DeviceIdType.MESH
F32 = jnp.float32
BF16 = jnp.bfloat16
SIDE = 4


def kernel(
    blk_ref, w_hbm, g_ref, child_ref,
    panel, tp, gb, part, parts_in,
    ring_send, ring_recv, pair_send, pair_recv, own_send, own_recv,
    t_send, t_recv, local_sem, p1_send, p1_recv, p2_send, p2_recv, rs_send, rs_recv,
):
    row = lax.axis_index("row")
    col = lax.axis_index("col")
    rows = lax.axis_size("row")
    cols = lax.axis_size("col")
    core = lax.rem(row, 2)
    z = row // 2
    x = col // SIDE
    y = lax.rem(col, SIDE)
    partner = row + 1 - 2 * core
    up = lax.rem(row + 2, rows)
    down = lax.rem(row + rows - 2, rows)
    diagonal = z == col
    wr, wc = w_hbm.shape
    half = wc // 2
    chunk = blk_ref.shape[0] // 2

    def copy(src, dst, ssem, rsem, r, c):
        return pltpu.make_async_remote_copy(
            src_ref=src, dst_ref=dst, send_sem=ssem, recv_sem=rsem,
            device_id=(r, c), device_id_type=MESH,
        )

    barrier = pltpu.get_barrier_semaphore()

    def greet(r, c):
        pl.semaphore_signal(barrier, inc=1, device_id=(r, c), device_id_type=MESH)

    for r in (up, down, partner):
        greet(r, col)
    for d in range(1, cols):
        greet(row, lax.rem(col + d, cols))
    @pl.when(jnp.logical_not(diagonal))
    def _():
        greet(2 * col, z)
        greet(2 * col + 1, z)

    pl.semaphore_wait(barrier, cols - 1 + 3 + jnp.where(diagonal, 0, 2))

    rows_of = lambda h: pl.ds(h * chunk, chunk)

    def ring(direction, step, h, src, slot):
        return copy(
            src, panel.at[slot, rows_of(h)],
            ring_send.at[direction, step, h], ring_recv.at[direction, step, h],
            up if direction == 0 else down, col,
        )

    def to_pair(direction, step, h, slot):
        return copy(
            panel.at[slot, rows_of(h)], panel.at[slot, rows_of(h)],
            pair_send.at[direction, step, h], pair_recv.at[direction, step, h],
            partner, col,
        )

    def own_pair(h):
        return copy(
            blk_ref.at[rows_of(h)], panel.at[row, rows_of(h)],
            own_send.at[h], own_recv.at[h], partner, col,
        )

    for h in range(2):
        for direction in range(2):
            ring(direction, 0, h, blk_ref.at[rows_of(h)], row).start()

    def mirrored(k):
        return copy(
            blk_ref.at[pl.ds(0, wr), pl.ds(k * half, half)],
            tp.at[z, pl.ds(pl.multiple_of(core * wr, wr), wr)],
            t_send.at[k], t_recv.at[core], 2 * col + k, z,
        )

    local = pltpu.make_async_copy(
        w_hbm.at[:, pl.ds(pl.multiple_of(core * half, half), half)],
        tp.at[col, pl.ds(pl.multiple_of(core * wr, wr), wr)],
        local_sem,
    )
    for k in range(2):
        mine = jnp.logical_and(diagonal, core == k)

        @pl.when(jnp.logical_not(mine))
        def _():
            mirrored(k).start()

    @pl.when(diagonal)
    def _():
        local.start()

    for h in range(2):
        own_pair(h).start()
    panel[row] = blk_ref[...]

    steps = rows // 4

    def ring_step(s):
        for h in range(2):
            for direction in range(2):
                off = 2 * s
                slot = lax.rem(row + (rows - off if direction == 0 else off), rows)

                def handle():
                    ring(direction, s - 1, h, panel.at[slot, rows_of(h)], slot).wait_recv()

                    @pl.when(jnp.logical_or(s + 1 < steps, jnp.logical_and(s + 1 == steps, h == direction)))
                    def _():
                        ring(direction, s, h, panel.at[slot, rows_of(h)], slot).start()

                    to_pair(direction, s - 1, h, slot).start()

                @pl.when(jnp.logical_or(s < steps, h == direction))
                def _():
                    handle()

    def ring_range(a, b):
        def step(s, carry):
            ring_step(s)
            return carry

        lax.fori_loop(a, b, step, 0)

    ring_range(1, 3)

    def part_rows(k):
        return pl.ds(k * wr, wr)

    for k in range(2):
        here = jnp.logical_and(diagonal, core == k)

        @pl.when(jnp.logical_not(here))
        def _():
            copy(
                blk_ref.at[pl.ds(0, wr), pl.ds(0, half)], tp.at[col, part_rows(k)],
                t_send.at[k], t_recv.at[k], 2 * col + k, z,
            ).wait_recv()

    @pl.when(diagonal)
    def _():
        local.wait()

    def moved(k, d):
        if k == 0:
            return lax.rem(x + d, SIDE) * SIDE + y
        return x * SIDE + lax.rem(y + d, SIDE)

    def first(k, d, slot):
        return copy(
            tp.at[slot, part_rows(k)], tp.at[slot, part_rows(k)],
            p1_send.at[k, d - 1], p1_recv.at[k, d - 1], row, moved(k, d),
        )

    def second(k, e, d, slot):
        return copy(
            tp.at[slot, part_rows(k)], tp.at[slot, part_rows(k)],
            p2_send.at[k, e, d - 1], p2_recv.at[k, e, d - 1], row, moved(1 - k, d),
        )

    order = (1, 3, 2)
    for d in order:
        for k in range(2):
            first(k, d, col).start()
    for d in order:
        for k in range(2):
            second(k, 0, d, col).start()
    ring_range(3, 5)
    for e in order:
        for k in range(2):
            slot = moved(k, SIDE - e)
            first(k, e, slot).wait_recv()
            for d in order:
                second(k, e, d, slot).start()
    ring_range(5, steps + 1)

    for e in range(SIDE):
        for k in range(2):
            for d in order:
                second(k, e, d, col).wait_recv()
    for h in range(2):
        own_pair(h).wait_recv()
    for s in range(1, steps + 1):
        for h in range(2):
            for direction in range(2):
                if s < steps or h == direction:
                    to_pair(direction, s - 1, h, row).wait_recv()

    def add(m, carry):
        left = tp[m]
        right = panel[pl.ds(2 * m, 2), pl.ds(0, wr)].reshape(2 * wr, wc)
        prod = lax.dot_general(left, right, (((0,), (0,)), ((), ())), preferred_element_type=F32)

        @pl.when(m == 0)
        def _():
            g_ref[...] = prod

        @pl.when(m > 0)
        def _():
            g_ref[...] += prod

        return carry

    lax.fori_loop(0, cols, add, 0)
    gb[...] = g_ref[...].astype(BF16)

    def child_part(c, carry):
        cpl = panel[pl.ds(2 * c, 2), pl.ds(wr, blk_ref.shape[0] - wr)].reshape(part.shape[1], wc)
        part[c] = lax.dot_general(
            cpl, gb[...], (((1,), (1,)), ((), ())), preferred_element_type=F32
        ).astype(BF16)
        return carry

    lax.fori_loop(0, cols, child_part, 0)

    def scatter(d):
        to = lax.rem(col + d, cols)
        return copy(part.at[to], parts_in.at[col], rs_send.at[d - 1], rs_recv.at[d - 1], row, to)

    for d in range(1, cols):
        scatter(d).start()
    child_ref[...] = -part[col].astype(F32)
    for d in range(1, cols):
        scatter(d).wait_recv()
        child_ref[...] -= parts_in[lax.rem(col + cols - d, cols)].astype(F32)

    for h in range(2):
        own_pair(h).wait_send()
    for s in range(0, steps):
        for h in range(2):
            for direction in range(2):
                if s + 1 < steps or h == direction:
                    ring(direction, s, h, blk_ref.at[rows_of(h)], row).wait_send()
                    to_pair(direction, s, h, row).wait_send()
    for k in range(2):
        mine = jnp.logical_and(diagonal, core == k)

        @pl.when(jnp.logical_not(mine))
        def _():
            mirrored(k).wait_send()

    for k in range(2):
        for d in order:
            first(k, d, col).wait_send()
            for e in range(SIDE):
                second(k, e, d, col).wait_send()
    for d in range(1, cols):
        scatter(d).wait_send()


def body(factor, sel_tiles, coupling):
    rows, cols = lax.axis_size("row"), lax.axis_size("col")
    wr, wc = factor.shape
    kc = coupling.shape[1]
    row_index = lax.axis_index("row")
    blk = jnp.concatenate([factor, coupling.T], axis=0)
    kb = rows * kc // cols
    dma = pltpu.SemaphoreType.DMA
    vm = pl.BlockSpec(memory_space=pltpu.VMEM)
    steps = rows // 4
    gram, child = pl.pallas_call(
        kernel,
        out_shape=(
            jax.ShapeDtypeStruct((wr, wc), F32),
            jax.ShapeDtypeStruct((kb, wr), F32),
        ),
        in_specs=[vm, pl.BlockSpec(memory_space=pl.ANY)],
        out_specs=(vm, vm),
        scratch_shapes=[
            pltpu.VMEM((rows, wr + kc, wc), BF16),
            pltpu.VMEM((cols, 2 * wr, wc // 2), BF16),
            pltpu.VMEM((wr, wc), BF16),
            pltpu.VMEM((cols, kb, wr), BF16),
            pltpu.VMEM((cols, kb, wr), BF16),
            dma((2, steps, 2)), dma((2, steps, 2)),
            dma((2, steps, 2)), dma((2, steps, 2)),
            dma((2,)), dma((2,)),
            dma((2,)), dma((2,)), dma,
            dma((2, SIDE - 1)), dma((2, SIDE - 1)),
            dma((2, SIDE, SIDE - 1)), dma((2, SIDE, SIDE - 1)),
            dma((cols - 1,)), dma((cols - 1,)),
        ],
        compiler_params=pltpu.CompilerParams(
            collective_id=0, has_side_effects=True, vmem_limit_bytes=48 * 2**20
        ),
    )(blk, factor)
    global_rows = row_index * wr + jnp.arange(wr, dtype=jnp.int32)
    member = jnp.any((global_rows // TILE)[:, None] == sel_tiles[None, :], axis=1)
    return gram, jnp.where(member[None, :], child, jnp.float32(0.0))


def solution(mesh):
    return jax.shard_map(
        body,
        mesh=mesh,
        in_specs=(P("row", "col"), P(), P("col", "row")),
        out_specs=(P("row", "col"), P("col", "row")),
        check_vma=False,
    )
```

time: 352 us -> 157 us (0.45)
  waiting for transfers between devices: 314 us -> 0 us
  Pallas kernels: 0 us -> 153 us
  between operations: 13.8 us -> 0.68 us
  matrix products: 9.31 us -> 0 us
  starting transfers between devices: 6.65 us -> 0 us
    all_gather x2 -> x0, waiting for transfers between devices: 154 us -> none  [the longest x1 86.6 us: body(): whole = lax.all_gather(factor, 'row', axis=0, tiled=True)]
    pallas_call x0 -> x1, Pallas kernels: none -> 153 us  [body(): pl.pallas_call(kernel, out_shape=(jax.ShapeDtypeStruct((wr, wc), F32), ja...]
    psum x1 -> x0, waiting for transfers between devices: 130 us -> none  [from_root(): return lax.psum(kept, axis)]
    all_to_all x1 -> x0, waiting for transfers between devices: 29.1 us -> none  [summed_on_arrival(): lax.all_to_all(in_blocks(value, dim, devices), axis, 0, 0, tiled=True)]
    dot_general x2 -> x0, matrix products: 9.31 us -> none  [the longest x1 6.99 us: body(): lax.dot_general(partner, whole, (((0,), (0,)), ((), ())), preferred_eleme...]
    all_to_all x1 -> x0, starting transfers between devices: 6.54 us -> none  [summed_on_arrival(): lax.all_to_all(in_blocks(value, dim, devices), axis, 0, 0, tiled=True)]
    select_n x2 -> x1, other arithmetic: 4.96 us -> 0.67 us  [body(): return (gram, jnp.where(member[None, :], child, jnp.float32(0.0)))]
  transfers between devices with their start and end apart: 4 -> 0, of which waited for: 4 -> 0; matrix products, arithmetic and copies ran while one was open for 2% -> 0% of each run, Pallas kernels for 0% -> 0%
where the time goes in v1:
time: 157 us
  Pallas kernels  153 us (97%)
  other arithmetic  1.82 us (1%)
    pallas_call x1, Pallas kernels, body(): pl.pallas_call(kernel, out_shape=(jax.ShapeDtypeStruct((wr, wc), F32), ja...  153 us

profile of v1, /device:TPU:1, one launch (start us, length us, event | category | flops | bytes accessed | tf_op | source)
XLA Modules:
  0.0 157.0 jit_solution(9538689507965352521)
XLA Ops:
  0.6 0.0 copy-start
  0.6 1.1 pad_maximum_fusion.blk_ref
  1.7 0.0 copy-done
  1.7 153.1 %shard_map.50 = (f32[256,512]{1,0:T(8,128)S(1)}, f32[128,256]{1,0:T(8,128)S(1)}) custom-call(bf16[320,512]{1,0:T(8,128)(2,1)S(1)} %pad_maximum_fusion.blk_ref, bf16[256,512]{1,0:T(8,128)(2,1)S(1)} %copy-done), custom_call_target="tpu_custom_call" | custom-call | tf_op jit(solution)/shard_map/pallas_call | solution.py:278
  154.8 0.0 copy-start.1
  154.8 0.6 copy-done.1
  155.4 0.1 compare_reduce_fusion
  155.5 0.7 broadcast_select_fusion
  156.2 0.8 copy.6
  (1 shorter events, 0.0 us)
Async XLA Ops:
  0.6 1.1 copy-start
  154.8 0.7 copy-start.1

commit v2 on v0

v2 whole, which is shorter than its diff:
```python
import jax
import jax.numpy as jnp
from jax import lax
from jax.experimental import pallas as pl
from jax.experimental.pallas import tpu as pltpu
from jax.sharding import PartitionSpec as P

TILE = 128
MESH = pl.DeviceIdType.MESH
F32 = jnp.float32
BF16 = jnp.bfloat16
SIDE = 4
N = SIDE * SIDE
FAR = N // 2
CUTS = 2
HOPS = 8
EARLY = 6


def both(*conditions):
    out = conditions[0]
    for c in conditions[1:]:
        out = jnp.logical_and(out, c)
    return out


def kernel(
    w_ref, ut_ref, w_hbm, g_ref, child_ref,
    panel, upanel, tp, stage, gb, part, parts_in,
    ring_send, ring_recv, u_send, u_recv, pair_send, pair_recv, upair_send, upair_recv,
    own_send, own_recv,
    leg1_send, leg1_recv, leg2_send, leg2_recv, local_sem,
    p1_send, p1_recv, p2_send, p2_recv, rs_send, rs_recv,
):
    row = lax.axis_index("row")
    col = lax.axis_index("col")
    rows = 2 * N
    core = lax.rem(row, 2)
    z = row // 2
    x = col // SIDE
    y = lax.rem(col, SIDE)
    other = 1 - core
    partner = 2 * z + other
    up = lax.rem(row + 2, rows)
    down = lax.rem(row + rows - 2, rows)
    wr, wc = w_ref.shape
    half = wc // 2
    chunk = wr // CUTS

    def copy(src, dst, ssem, rsem, r, c):
        return pltpu.make_async_remote_copy(
            src_ref=src, dst_ref=dst, send_sem=ssem, recv_sem=rsem,
            device_id=(r, c), device_id_type=MESH,
        )

    reach = FAR

    def travels(m, direction, s, h):
        high = m >= N - reach
        if direction == 0:
            near = s < N - reach if h % 2 else s <= N - reach
            return both(m >= col, high, near)
        near = s <= reach if h % 2 else s < reach
        return both(m >= col, s <= m, jnp.logical_or(jnp.logical_not(high), near))

    def comes_at(m):
        down_only = jnp.logical_or(m < N - reach, m - z < reach)
        return jnp.where(down_only, m - z, N - (m - z))

    def wanted(m):
        return both(m >= col, m >= z)

    def origin(direction, s):
        return lax.rem(z + (N - s if direction == 0 else s), N)

    barrier = pltpu.get_barrier_semaphore()

    def greet(r, c):
        pl.semaphore_signal(barrier, inc=1, device_id=(r, c), device_id_type=MESH)

    turn = lax.rem(col + 2 * N - z - FAR * core, N)
    for r in (up, down, partner):
        greet(r, col)
    for d in range(1, N):
        greet(row, lax.rem(col + d, N))
    greet(partner, turn)

    @pl.when(turn != z)
    def _():
        greet(2 * turn + core, col)

    with jax.named_scope("barrier"):
        pl.semaphore_wait(barrier, N + 3 + jnp.where(turn != z, 1, 0))

    def rows_of(h):
        return pl.ds(h * chunk, chunk)

    def towards(direction):
        return up if direction == 0 else down

    def slot_of(m):
        return 2 * m + core

    def hop(direction, s, h, m, first):
        dst = panel.at[slot_of(m), rows_of(h)]
        return copy(
            w_ref.at[rows_of(h)] if first else dst, dst,
            ring_send.at[direction, s - 1, h], ring_recv.at[direction, s - 1, h], towards(direction), col,
        )

    def u_hop(direction, s, m, first):
        dst = upanel.at[slot_of(m)]
        return copy(
            ut_ref if first else dst, dst, u_send.at[direction, s - 1], u_recv.at[direction, s - 1],
            towards(direction), col,
        )

    def to_pair(direction, s, h, m):
        ref = panel.at[slot_of(m), rows_of(h)]
        return copy(
            ref, ref, pair_send.at[direction, s - 1, h], pair_recv.at[direction, s - 1, h], partner, col
        )

    def u_pair(direction, s, m):
        ref = upanel.at[slot_of(m)]
        return copy(ref, ref, upair_send.at[direction, s - 1], upair_recv.at[direction, s - 1], partner, col)

    def own_pair(k):
        src, dst = ((w_ref, panel), (ut_ref, upanel))[k]
        return copy(src, dst.at[row], own_send.at[k], own_recv.at[k], partner, col)

    def part_rows(k):
        return pl.ds(k * wr, wr)

    my_rows = pl.ds(pl.multiple_of(core * wr, wr), wr)

    def leg1(k, dst):
        to = lax.rem(z + col + FAR * k, N)
        return copy(
            w_ref.at[:, pl.ds(k * half, half)], dst, leg1_send.at[k], leg1_recv.at[core], 2 * z + k, to
        )

    def leg1_local(dst):
        return pltpu.make_async_copy(
            w_hbm.at[:, pl.ds(pl.multiple_of(core * half, half), half)], dst, local_sem
        )

    def leg1_self(k):
        return both(core == k, lax.rem(z + FAR * k, N) == 0)

    def leg2():
        return copy(stage, tp.at[z], leg2_send, leg2_recv, 2 * turn + core, col)

    for h in range(CUTS):
        for direction in range(2):
            @pl.when(travels(z, direction, 1, h))
            def _():
                hop(direction, 1, h, z, True).start()

    for k in range(2):
        for at_home in (False, True):
            dst = tp.at[z, my_rows] if at_home else stage.at[my_rows]
            good = both(z >= col, (z == col) == at_home)

            @pl.when(both(good, jnp.logical_not(leg1_self(k))))
            def _():
                leg1(k, dst).start()

            @pl.when(both(good, leg1_self(k)))
            def _():
                leg1_local(dst).start()

    for direction in range(2):
        u_hop(direction, 1, z, True).start()
    for k in range(2):
        own_pair(k).start()
    panel[row] = w_ref[...]
    upanel[row] = ut_ref[...]
    g_ref[...] = jnp.zeros_like(g_ref)

    def leg1_arrived():
        for k in range(2):
            here = both(turn == col, core == k)

            @pl.when(here)
            def _():
                leg1_local(stage.at[part_rows(k)]).wait()

            @pl.when(jnp.logical_not(here))
            def _():
                copy(
                    w_ref.at[:, pl.ds(0, half)], stage.at[part_rows(k)], leg1_send.at[k], leg1_recv.at[k],
                    row, col,
                ).wait_recv()

    def passes(s):
        for h in range(CUTS):
            for direction in range(2):
                m = origin(direction, s)

                @pl.when(travels(m, direction, s, h))
                def _():
                    hop(direction, s, h, m, False).wait_recv()

                    @pl.when(both(s < HOPS, travels(m, direction, s + 1, h)))
                    def _():
                        hop(direction, s + 1, h, m, False).start()

                    @pl.when(wanted(m))
                    def _():
                        to_pair(direction, s, h, m).start()

    def u_passes(s):
        for direction in range(2):
            m = origin(direction, s)

            @pl.when(s < FAR + 1 - direction)
            def _():
                u_hop(direction, s, m, False).wait_recv()

                @pl.when(s < FAR - direction)
                def _():
                    u_hop(direction, s + 1, m, False).start()

                u_pair(direction, s, m).start()

    def ring_step(s, carry):
        passes(s)
        u_passes(s)
        return carry

    def ring_range(a, b):
        with jax.named_scope("ring%d" % a):
            lax.fori_loop(a, b, ring_step, 0)

    ring_range(1, 2)

    @pl.when(z >= turn)
    def _():
        with jax.named_scope("leg1"):
            leg1_arrived()

        @pl.when(z > turn)
        def _():
            leg2().start()

    ring_range(2, 4)

    def moved(k, d):
        if k == 0:
            return lax.rem(x + d, SIDE) * SIDE + y
        return x * SIDE + lax.rem(y + d, SIDE)

    def row_of(c):
        return lax.rem(c + 2 * N - z - FAR * core, N)

    def least(k, c):
        return c // SIDE * SIDE if k == 0 else lax.rem(c, SIDE)

    def first(k, d, m):
        ref = tp.at[m, part_rows(k)]
        return copy(ref, ref, p1_send.at[k, d - 1], p1_recv.at[k, d - 1], row, moved(k, d))

    def second(k, e, d, m):
        ref = tp.at[m, part_rows(k)]
        return copy(ref, ref, p2_send.at[k, e, d - 1], p2_recv.at[k, e, d - 1], row, moved(1 - k, d))

    def first_goes(k, m, c):
        return both(m >= z, m >= least(k, c))

    def second_goes(m, c):
        return both(m >= z, m >= c)

    order = (1, 3, 2)
    mine = turn

    @pl.when(mine > z)
    def _():
        with jax.named_scope("leg2"):
            copy(stage, tp.at[mine], leg2_send, leg2_recv, row, col).wait_recv()

    for d in order:
        for k in range(2):
            @pl.when(first_goes(k, mine, moved(k, d)))
            def _():
                first(k, d, mine).start()
    for d in order:
        for k in range(2):
            @pl.when(second_goes(mine, moved(1 - k, d)))
            def _():
                second(k, 0, d, mine).start()

    ring_range(4, 6)

    for e in order:
        for k in range(2):
            m = row_of(moved(k, SIDE - e))

            @pl.when(first_goes(k, m, col))
            def _():
                with jax.named_scope("first%d%d" % (k, e)):
                    first(k, e, m).wait_recv()
                for d in order:
                    @pl.when(second_goes(m, moved(1 - k, d)))
                    def _():
                        second(k, e, d, m).start()

    ring_range(6, EARLY + 2)

    with jax.named_scope("second"):
        for e in range(SIDE):
            for k in range(2):
                for d in order:
                    a, b = (e, d) if k == 0 else (d, e)
                    c = lax.rem(x + SIDE - a, SIDE) * SIDE + lax.rem(y + SIDE - b, SIDE)
                    m = row_of(c)

                    @pl.when(second_goes(m, col))
                    def _():
                        second(k, e, d, m).wait_recv()

    def pairs(s, carry):
        for h in range(CUTS):
            for direction in range(2):
                m = origin(direction, s)

                @pl.when(both(travels(m, direction, s, h), wanted(m)))
                def _():
                    to_pair(direction, s, h, m).wait_recv()

        return carry

    def add(m):
        left = tp[m]
        right = panel[pl.ds(2 * m, 2)].reshape(2 * wr, wc)
        g_ref[...] += lax.dot_general(left, right, (((0,), (0,)), ((), ())), preferred_element_type=F32)

    with jax.named_scope("pairs"):
        for k in range(2):
            own_pair(k).wait_recv()
        lax.fori_loop(1, EARLY + 1, pairs, 0)

    def add_blocks(early):
        def step(m, carry):
            @pl.when(both(wanted(m), (comes_at(m) <= EARLY) == early))
            def _():
                add(m)

            return carry

        lax.fori_loop(0, N, step, 0)

    with jax.named_scope("gram"):
        add_blocks(True)

    ring_range(EARLY + 2, HOPS + 1)

    with jax.named_scope("last"):
        lax.fori_loop(EARLY + 1, HOPS + 1, pairs, 0)
        add_blocks(False)
        for direction in range(2):
            for s in range(1, FAR + 1 - direction):
                u_pair(direction, s, origin(direction, s)).wait_recv()
    gb[...] = jnp.transpose(g_ref[...].astype(BF16))

    def child_part(c, carry):
        cpl = upanel[pl.ds(8 * c, 8)].reshape(4 * part.shape[1], wc)
        prod = jnp.dot(cpl, gb[...], preferred_element_type=F32).astype(BF16)
        part[pl.ds(4 * c, 4)] = prod.reshape(4, *part.shape[1:])
        return carry

    with jax.named_scope("child"):
        lax.fori_loop(0, N // 4, child_part, 0)

    def scatter(d):
        to = lax.rem(col + d, N)
        return copy(part.at[to], parts_in.at[col], rs_send.at[d - 1], rs_recv.at[d - 1], row, to)

    for d in range(1, N):
        scatter(d).start()
    def sent(s, carry):
        for direction in range(2):
            m = origin(direction, s - 1)
            got = origin(direction, s)
            for h in range(CUTS):
                @pl.when(travels(m, direction, s, h))
                def _():
                    hop(direction, s, h, m, False).wait_send()

                @pl.when(both(travels(got, direction, s, h), wanted(got)))
                def _():
                    to_pair(direction, s, h, got).wait_send()

            @pl.when(s < FAR + 1 - direction)
            def _():
                u_hop(direction, s, m, False).wait_send()
                u_pair(direction, s, got).wait_send()

        return carry

    with jax.named_scope("sends"):
        lax.fori_loop(1, HOPS + 1, sent, 0)
        for k in range(2):
            own_pair(k).wait_send()

            @pl.when(both(z >= col, jnp.logical_not(leg1_self(k))))
            def _():
                leg1(k, stage.at[my_rows]).wait_send()

            for d in order:
                @pl.when(first_goes(k, mine, moved(k, d)))
                def _():
                    first(k, d, mine).wait_send()

                for e in range(SIDE):
                    m = row_of(moved(k, SIDE - e if e else 0))
                    reaches = second_goes(m, moved(1 - k, d))

                    @pl.when(reaches)
                    def _():
                        second(k, e, d, m).wait_send()

        @pl.when(z > turn)
        def _():
            leg2().wait_send()


    with jax.named_scope("scatter"):
        child_ref[...] = -part[col].astype(F32)
        for d in range(1, N):
            scatter(d).wait_recv()
            child_ref[...] -= parts_in[lax.rem(col + N - d, N)].astype(F32)
        for d in range(1, N):
            scatter(d).wait_send()


def body(factor, sel_tiles, coupling):
    rows, cols = lax.axis_size("row"), lax.axis_size("col")
    assert rows == 2 * N and cols == N
    wr, wc = factor.shape
    kc = coupling.shape[1]
    row_index = lax.axis_index("row")
    kb = rows * kc // cols
    dma = pltpu.SemaphoreType.DMA
    vm = pl.BlockSpec(memory_space=pltpu.VMEM)
    pair_of = lambda *shape: [dma(shape), dma(shape)]
    gram, child = pl.pallas_call(
        kernel,
        out_shape=(
            jax.ShapeDtypeStruct((wr, wc), F32),
            jax.ShapeDtypeStruct((kb, wr), F32),
        ),
        in_specs=[vm, vm, pl.BlockSpec(memory_space=pl.ANY)],
        out_specs=(vm, vm),
        scratch_shapes=[
            pltpu.VMEM((rows, wr, wc), BF16),
            pltpu.VMEM((rows, kc, wc), BF16),
            pltpu.VMEM((cols, 2 * wr, wc // 2), BF16),
            pltpu.VMEM((2 * wr, wc // 2), BF16),
            pltpu.VMEM((wc, wr), BF16),
            pltpu.VMEM((cols, kb, wr), BF16),
            pltpu.VMEM((cols, kb, wr), BF16),
            *pair_of(2, HOPS, CUTS), *pair_of(2, FAR), *pair_of(2, HOPS, CUTS), *pair_of(2, FAR),
            *pair_of(2),
            *pair_of(2), dma, dma, dma,
            *pair_of(2, SIDE - 1), *pair_of(2, SIDE, SIDE - 1), *pair_of(cols - 1),
        ],
        compiler_params=pltpu.CompilerParams(
            collective_id=0, has_side_effects=True, vmem_limit_bytes=52 * 2**20
        ),
    )(factor, coupling.T, factor)
    global_rows = row_index * wr + jnp.arange(wr, dtype=jnp.int32)
    member = jnp.any((global_rows // TILE)[:, None] == sel_tiles[None, :], axis=1)
    return gram, jnp.where(member[None, :], child, jnp.float32(0.0))


def solution(mesh):
    return jax.shard_map(
        body,
        mesh=mesh,
        in_specs=(P("row", "col"), P(), P("col", "row")),
        out_specs=(P("row", "col"), P("col", "row")),
        check_vma=False,
    )
```

time: 352 us -> 111 us (0.32)
  waiting for transfers between devices: 314 us -> 0 us
  Pallas kernels: 0 us -> 106 us
  between operations: 13.8 us -> 0.67 us
  matrix products: 9.31 us -> 0 us
  starting transfers between devices: 6.65 us -> 0 us
  other arithmetic: 5.17 us -> 0.77 us
    all_gather x2 -> x0, waiting for transfers between devices: 154 us -> none  [the longest x1 86.6 us: body(): whole = lax.all_gather(factor, 'row', axis=0, tiled=True)]
    psum x1 -> x0, waiting for transfers between devices: 130 us -> none  [from_root(): return lax.psum(kept, axis)]
    pallas_call x0 -> x1, Pallas kernels: none -> 106 us  [body(): pl.pallas_call(kernel, out_shape=(jax.ShapeDtypeStruct((wr, wc), F32), ja...]
    all_to_all x1 -> x0, waiting for transfers between devices: 29.1 us -> none  [summed_on_arrival(): lax.all_to_all(in_blocks(value, dim, devices), axis, 0, 0, tiled=True)]
    dot_general x2 -> x0, matrix products: 9.31 us -> none  [the longest x1 6.99 us: body(): lax.dot_general(partner, whole, (((0,), (0,)), ((), ())), preferred_eleme...]
    all_to_all x1 -> x0, starting transfers between devices: 6.54 us -> none  [summed_on_arrival(): lax.all_to_all(in_blocks(value, dim, devices), axis, 0, 0, tiled=True)]
    select_n x2 -> x1, other arithmetic: 4.96 us -> 0.67 us  [body(): return (gram, jnp.where(member[None, :], child, jnp.float32(0.0)))]
  transfers between devices with their start and end apart: 4 -> 0, of which waited for: 4 -> 0; matrix products, arithmetic and copies ran while one was open for 2% -> 0% of each run, Pallas kernels for 0% -> 0%
where the time goes in v2:
time: 111 us; the launch traced here: 110 us
  Pallas kernels  106 us (95%)
  local copies, waits for them, and re-layouts  3.21 us (3%)
    pallas_call x1, Pallas kernels, body(): pl.pallas_call(kernel, out_shape=(jax.ShapeDtypeStruct((wr, wc), F32), ja...  106 us
    unnamed x7, local copies, waits for them, and re-layouts  3.21 us

profile of v2, /device:TPU:1, one launch (start us, length us, event | category | flops | bytes accessed | tf_op | source)
XLA Modules:
  0.0 110.3 jit_solution(15452605035259452586)
XLA Ops:
  0.6 0.0 copy-start
  0.6 0.9 copy-done
  1.6 0.0 copy-start.1
  1.6 0.8 copy-done.1
  2.4 105.7 %shard_map.50 = (f32[256,512]{1,0:T(8,128)S(1)}, f32[128,256]{1,0:T(8,128)S(1)}) custom-call(bf16[256,512]{1,0:T(8,128)(2,1)S(1)} %copy-done, bf16[64,512]{1,0:T(8,128)(2,1)S(1)} %bitcast.1, bf16[256,512]{1,0:T(8,128)(2,1)S(1)} %copy-done), custom_call_target="tpu_custom_call" | custom-call | tf_op jit(solution)/shard_map/pallas_call | solution.py:447
  108.1 0.0 copy-start.2
  108.2 0.6 copy-done.2
  108.8 0.1 compare_reduce_fusion
  108.9 0.7 broadcast_select_fusion
  109.5 0.8 copy.6
  (1 shorter events, 0.0 us)
Async XLA Ops:
  0.6 1.0 copy-start
  1.6 0.8 copy-start.1
  108.1 0.7 copy-start.2

commit v3 on v2

v3 whole, which is shorter than its diff:
```python
import jax
import jax.numpy as jnp
from jax import lax
from jax.experimental import pallas as pl
from jax.experimental.pallas import tpu as pltpu
from jax.sharding import PartitionSpec as P

TILE = 128
MESH = pl.DeviceIdType.MESH
F32 = jnp.float32
BF16 = jnp.bfloat16
SIDE = 4
N = SIDE * SIDE
FAR = N // 2
CUTS = 2
HOPS = FAR
NEAR = 4
MIRRORED = 4
EARLY = 5


def both(*conditions):
    out = conditions[0]
    for c in conditions[1:]:
        out = jnp.logical_and(out, c)
    return out


def kernel(
    w_ref, ut_ref, member_ref, g_ref, child_ref,
    panel, upanel, tp, stage, gb, part, sums, mids, row_in, last_in,
    ring_send, ring_recv, u_send, u_recv, pair_send, pair_recv, upair_send, upair_recv,
    own_send, own_recv,
    leg1_send, leg1_recv, leg2_send, leg2_recv, hand_send, hand_recv, hand_own,
    p1_send, p1_recv, p2_send, p2_recv, r1_send, r1_recv, r2_send, r2_recv,
):
    row = lax.axis_index("row")
    col = lax.axis_index("col")
    rows = 2 * N
    core = lax.rem(row, 2)
    z = row // 2
    x = col // SIDE
    y = lax.rem(col, SIDE)
    other = 1 - core
    partner = 2 * z + other
    up = lax.rem(row + 2, rows)
    down = lax.rem(row + rows - 2, rows)
    wr, wc = w_ref.shape
    half = wc // 2
    chunk = wr // CUTS

    def copy(src, dst, ssem, rsem, r, c):
        return pltpu.make_async_remote_copy(
            src_ref=src, dst_ref=dst, send_sem=ssem, recv_sem=rsem,
            device_id=(r, c), device_id_type=MESH,
        )

    def travels(m, direction, s, h):
        near = jnp.logical_or(s < FAR, h % 2 == direction)
        return both(m >= col, m >= FAR if direction == 0 else s <= m, near)

    def gap(m, plane):
        return jnp.where(m - plane <= FAR, m - plane, N - (m - plane))

    def comes_at(m):
        return gap(m, z)

    def wanted(m):
        return both(m >= col, m >= z)

    def origin(direction, s):
        return lax.rem(z + (N - s if direction == 0 else s), N)

    barrier = pltpu.get_barrier_semaphore()

    def greet(r, c):
        pl.semaphore_signal(barrier, inc=1, device_id=(r, c), device_id_type=MESH)

    turn = lax.rem(col + 2 * N - z - FAR * core, N)
    for r in (up, down, partner):
        greet(r, col)
    for d in range(1, N):
        greet(row, lax.rem(col + d, N))
    greet(partner, turn)

    @pl.when(turn != z)
    def _():
        greet(2 * turn + core, col)

    @pl.when(col != z)
    def _():
        greet(partner, z)

    with jax.named_scope("barrier"):
        pl.semaphore_wait(barrier, N + 3 + jnp.where(turn != z, 1, 0) + jnp.where(col == z, N - 1, 0))

    def rows_of(h):
        return pl.ds(h * chunk, chunk)

    def towards(direction):
        return up if direction == 0 else down

    def slot_of(m):
        return 2 * m + core

    def hop(direction, s, h, m, first):
        dst = panel.at[slot_of(m), rows_of(h)]
        return copy(
            w_ref.at[rows_of(h)] if first else dst, dst,
            ring_send.at[direction, s - 1, h], ring_recv.at[direction, s - 1, h], towards(direction), col,
        )

    def u_hop(direction, s, m, first):
        dst = upanel.at[slot_of(m)]
        return copy(
            ut_ref if first else dst, dst, u_send.at[direction, s - 1], u_recv.at[direction, s - 1],
            towards(direction), col,
        )

    def to_pair(direction, s, h, m):
        ref = panel.at[slot_of(m), rows_of(h)]
        return copy(
            ref, ref, pair_send.at[direction, s - 1, h], pair_recv.at[direction, s - 1, h], partner, col
        )

    def u_pair(direction, s, m):
        ref = upanel.at[slot_of(m)]
        return copy(ref, ref, upair_send.at[direction, s - 1], upair_recv.at[direction, s - 1], partner, col)

    def own_pair(k):
        src, dst = ((w_ref, panel), (ut_ref, upanel))[k]
        return copy(src, dst.at[row], own_send.at[k], own_recv.at[k], partner, col)

    def part_rows(k):
        return pl.ds(k * wr, wr)

    my_rows = pl.ds(pl.multiple_of(core * wr, wr), wr)

    def leg1(k, dst):
        to = lax.rem(z + col + FAR * k, N)
        return copy(
            w_ref.at[:, pl.ds(k * half, half)], dst, leg1_send.at[k], leg1_recv.at[core], 2 * z + k, to
        )

    def stays(k, m):
        return both(core == k, lax.rem(m + FAR * k, N) == 0)

    def mirrors(m, plane):
        return both(m >= plane, gap(m, plane) > NEAR)

    def leg2():
        return copy(stage, tp.at[z], leg2_send, leg2_recv, 2 * turn + core, col)

    for h in range(CUTS):
        for direction in range(2):
            @pl.when(travels(z, direction, 1, h))
            def _():
                hop(direction, 1, h, z, True).start()

    for k in range(2):
        @pl.when(both(mirrors(z, col), jnp.logical_not(stays(k, z))))
        def _():
            leg1(k, stage.at[my_rows]).start()

        @pl.when(both(mirrors(z, col), stays(k, z)))
        def _():
            stage[my_rows] = w_ref[:, pl.ds(k * half, half)]

    def hand(k, h, m, src, sem):
        return copy(
            src.at[:, pl.ds(k * half, half)],
            tp.at[m, pl.ds(pl.multiple_of(core * wr + h * chunk, chunk), chunk)],
            sem, hand_recv.at[core, h], 2 * z + k, lax.rem(m + z + FAR * k, N),
        )

    def hands(h, m, src, sem_of):
        for k in range(2):
            @pl.when(stays(k, m))
            def _():
                tp[m, pl.ds(pl.multiple_of(core * wr + h * chunk, chunk), chunk)] = src[:, pl.ds(k * half, half)]

            @pl.when(jnp.logical_not(stays(k, m)))
            def _():
                hand(k, h, m, src, sem_of(k)).start()

    @pl.when(col == z)
    def _():
        for h in range(CUTS):
            hands(h, z, w_ref.at[rows_of(h)], lambda k: hand_own.at[h, k])

    for direction in range(2):
        u_hop(direction, 1, z, True).start()
    for k in range(2):
        own_pair(k).start()
    panel[row] = w_ref[...]
    upanel[row] = ut_ref[...]
    g_ref[...] = jnp.zeros_like(g_ref)

    def leg1_arrived():
        for k in range(2):
            @pl.when(jnp.logical_not(both(turn == col, core == k)))
            def _():
                copy(
                    w_ref.at[:, pl.ds(0, half)], stage.at[part_rows(k)], leg1_send.at[k], leg1_recv.at[k],
                    row, col,
                ).wait_recv()

    def moved(k, d):
        if k == 0:
            return lax.rem(x + d, SIDE) * SIDE + y
        return x * SIDE + lax.rem(y + d, SIDE)

    def row_of(c):
        return lax.rem(c + 2 * N - z - FAR * core, N)

    def least(k, c):
        return c // SIDE * SIDE if k == 0 else lax.rem(c, SIDE)

    def first(k, d, m):
        ref = tp.at[m, part_rows(k)]
        return copy(ref, ref, p1_send.at[k, d - 1], p1_recv.at[k, d - 1], row, moved(k, d))

    def second(k, e, d, m):
        ref = tp.at[m, part_rows(k)]
        return copy(ref, ref, p2_send.at[k, e, d - 1], p2_recv.at[k, e, d - 1], row, moved(1 - k, d))

    def first_goes(k, m, c):
        return both(m >= z, m >= least(k, c))

    def second_goes(m, c):
        return both(m >= z, m >= c)

    order = (1, 3, 2)
    mine = turn

    def first_all(action):
        for d in order:
            for k in range(2):
                @pl.when(first_goes(k, mine, moved(k, d)))
                def _():
                    action(first(k, d, mine))

    def second_all(k, e, m, action):
        for d in order:
            @pl.when(second_goes(m, moved(1 - k, d)))
            def _():
                action(second(k, e, d, m))

    def starts_at(m):
        return jnp.where(comes_at(m) <= NEAR, comes_at(m) + 1, MIRRORED)

    def spread(s):
        @pl.when(both(mine >= z, starts_at(mine) == s))
        def _():
            @pl.when(mirrors(mine, z))
            def _():
                copy(stage, tp.at[mine], leg2_send, leg2_recv, row, col).wait_recv()

            for k in range(2):
                @pl.when(jnp.logical_not(jnp.logical_or(mirrors(mine, z), both(col == z, core == k))))
                def _():
                    for h in range(CUTS):
                        pltpu.make_async_remote_copy(
                            src_ref=w_ref.at[rows_of(h), pl.ds(0, half)],
                            dst_ref=tp.at[mine, pl.ds(k * wr + h * chunk, chunk)],
                            send_sem=hand_own.at[h, k], recv_sem=hand_recv.at[k, h],
                            device_id=(partner, col), device_id_type=MESH,
                        ).wait_recv()

            first_all(lambda c: c.start())
            for k in range(2):
                second_all(k, 0, mine, lambda c: c.start())

    def relay(s):
        for e in order:
            for k in range(2):
                m = row_of(moved(k, SIDE - e))

                @pl.when(both(starts_at(m) + 1 == s, first_goes(k, m, col)))
                def _():
                    first(k, e, m).wait_recv()
                    second_all(k, e, m, lambda c: c.start())

    def passes(s):
        for h in range(CUTS):
            for direction in range(2):
                m = origin(direction, s)

                @pl.when(travels(m, direction, s, h))
                def _():
                    hop(direction, s, h, m, False).wait_recv()

                    @pl.when(both(s < HOPS, travels(m, direction, s + 1, h)))
                    def _():
                        hop(direction, s + 1, h, m, False).start()

                    @pl.when(wanted(m))
                    def _():
                        to_pair(direction, s, h, m).start()

                    @pl.when(both(col == z, m >= z, s <= NEAR))
                    def _():
                        src = panel.at[slot_of(m), rows_of(h)]
                        hands(h, m, src, lambda k: hand_send.at[direction, s - 1, h, k])

    def u_passes(s):
        for direction in range(2):
            m = origin(direction, s)

            @pl.when(s < FAR + 1 - direction)
            def _():
                u_hop(direction, s, m, False).wait_recv()

                @pl.when(s < FAR - direction)
                def _():
                    u_hop(direction, s + 1, m, False).start()

                u_pair(direction, s, m).start()

    def ring_step(s, carry):
        passes(s)
        u_passes(s)
        spread(s)
        relay(s)
        return carry

    def ring_range(a, b):
        with jax.named_scope("ring%d" % a):
            lax.fori_loop(a, b, ring_step, 0)

    ring_range(1, 2)

    @pl.when(mirrors(z, turn))
    def _():
        with jax.named_scope("leg1"):
            leg1_arrived()
        leg2().start()

    for a in range(2, HOPS + 1, 2):
        ring_range(a, min(a + 2, HOPS + 1))

    def spreads(early):
        for e in range(SIDE):
            for k in range(2):
                for d in order:
                    a, b = (e, d) if k == 0 else (d, e)
                    c = lax.rem(x + SIDE - a, SIDE) * SIDE + lax.rem(y + SIDE - b, SIDE)
                    m = row_of(c)

                    @pl.when(both((comes_at(m) <= EARLY) == early, second_goes(m, col)))
                    def _():
                        second(k, e, d, m).wait_recv()

    def pairs(s, carry):
        for h in range(CUTS):
            for direction in range(2):
                m = origin(direction, s)

                @pl.when(both(travels(m, direction, s, h), wanted(m)))
                def _():
                    to_pair(direction, s, h, m).wait_recv()

        return carry

    def add(m):
        left = tp[m]
        right = panel[pl.ds(2 * m, 2)].reshape(2 * wr, wc)
        g_ref[...] += lax.dot_general(left, right, (((0,), (0,)), ((), ())), preferred_element_type=F32)

    with jax.named_scope("pairs"):
        spreads(True)
        for k in range(2):
            own_pair(k).wait_recv()
        lax.fori_loop(1, EARLY + 1, pairs, 0)

    def add_blocks(early):
        def step(m, carry):
            @pl.when(both(wanted(m), (comes_at(m) <= EARLY) == early))
            def _():
                add(m)

            return carry

        lax.fori_loop(0, N, step, 0)

    with jax.named_scope("gram"):
        add_blocks(True)

    with jax.named_scope("last"):
        spreads(False)
        lax.fori_loop(EARLY + 1, HOPS + 1, pairs, 0)
        add_blocks(False)
        for direction in range(2):
            for s in range(1, FAR + 1 - direction):
                u_pair(direction, s, origin(direction, s)).wait_recv()
    gb[...] = jnp.transpose(g_ref[...].astype(BF16))

    lanes = wr // 2

    def half_of(k):
        return pl.ds(k * lanes, lanes)

    def line(ref, k, i):
        return ref.at[i, :, :, half_of(k)] if k == 0 else ref.at[:, i, :, half_of(k)]

    def place(k, d):
        return lax.rem((y if k else x) + d, SIDE)

    def reduce1(k, d):
        return copy(
            line(part, k, place(k, d)), row_in.at[k, d - 1], r1_send.at[k, d - 1], r1_recv.at[k, d - 1],
            row, moved(k, d),
        )

    def reduce2(k, d):
        return copy(
            mids.at[k, place(1 - k, d)], last_in.at[k, d - 1], r2_send.at[k, d - 1], r2_recv.at[k, d - 1],
            row, moved(1 - k, d),
        )

    def child_part(i, carry):
        cpl = upanel[pl.ds(2 * SIDE * i, 2 * SIDE)].reshape(SIDE * part.shape[2], wc)
        prod = jnp.dot(cpl, gb[...], preferred_element_type=F32).astype(BF16)
        part[i] = prod.reshape(SIDE, *part.shape[2:])
        return carry

    with jax.named_scope("child"):
        lax.fori_loop(0, SIDE, child_part, 0)
    for d in order:
        for k in range(2):
            reduce1(k, d).start()

    def sent(s, carry):
        for direction in range(2):
            m = origin(direction, s - 1)
            got = origin(direction, s)
            for h in range(CUTS):
                @pl.when(travels(m, direction, s, h))
                def _():
                    hop(direction, s, h, m, False).wait_send()

                @pl.when(both(travels(got, direction, s, h), wanted(got)))
                def _():
                    to_pair(direction, s, h, got).wait_send()

            @pl.when(s < FAR + 1 - direction)
            def _():
                u_hop(direction, s, m, False).wait_send()
                u_pair(direction, s, got).wait_send()

        return carry

    with jax.named_scope("sends"):
        lax.fori_loop(1, HOPS + 1, sent, 0)
        for k in range(2):
            own_pair(k).wait_send()

            @pl.when(both(mirrors(z, col), jnp.logical_not(stays(k, z))))
            def _():
                leg1(k, stage.at[my_rows]).wait_send()

            for e in range(SIDE):
                second_all(k, e, row_of(moved(k, SIDE - e if e else 0)), lambda c: c.wait_send())

        first_all(lambda c: c.wait_send())

        @pl.when(mirrors(z, turn))
        def _():
            leg2().wait_send()

        def handed(h, m, sem_of):
            for k in range(2):
                @pl.when(jnp.logical_not(stays(k, m)))
                def _():
                    hand(k, h, m, w_ref.at[rows_of(h)], sem_of(k)).wait_send()

        @pl.when(col == z)
        def _():
            for h in range(CUTS):
                handed(h, z, lambda k: hand_own.at[h, k])

            def handed_on(s, carry):
                for h in range(CUTS):
                    for direction in range(2):
                        m = origin(direction, s)

                        @pl.when(both(travels(m, direction, s, h), m >= z))
                        def _():
                            handed(h, m, lambda k: hand_send.at[direction, s - 1, h, k])

                return carry

            lax.fori_loop(1, NEAR + 1, handed_on, 0)

    with jax.named_scope("reduce1"):
        for k in range(2):
            mine = part[x, :, :, half_of(k)] if k == 0 else part[:, y, :, half_of(k)]
            sums[k] = mine.astype(F32)
            for d in order:
                reduce1(k, d).wait_recv()
                sums[k] += row_in[k, d - 1].astype(F32)
            mids[k] = sums[k].astype(BF16)
            for d in order:
                reduce2(k, d).start()
    with jax.named_scope("reduce2"):
        for k in range(2):
            total = sums[k, y if k == 0 else x]
            for d in order:
                reduce2(k, d).wait_recv()
                total += last_in[k, d - 1].astype(F32)
            child_ref[:, half_of(k)] = jnp.where(member_ref[:, half_of(k)] > 0, -total, 0.0)
        for k in range(2):
            for d in order:
                reduce1(k, d).wait_send()
                reduce2(k, d).wait_send()


def body(factor, sel_tiles, coupling):
    rows, cols = lax.axis_size("row"), lax.axis_size("col")
    assert rows == 2 * N and cols == N
    wr, wc = factor.shape
    kc = coupling.shape[1]
    row_index = lax.axis_index("row")
    kb = rows * kc // cols
    dma = pltpu.SemaphoreType.DMA
    vm = pl.BlockSpec(memory_space=pltpu.VMEM)
    global_rows = row_index * wr + jnp.arange(wr, dtype=jnp.int32)
    member = jnp.any((global_rows // TILE)[:, None] == sel_tiles[None, :], axis=1)
    pair_of = lambda *shape: [dma(shape), dma(shape)]
    gram, child = pl.pallas_call(
        kernel,
        out_shape=(
            jax.ShapeDtypeStruct((wr, wc), F32),
            jax.ShapeDtypeStruct((kb, wr), F32),
        ),
        in_specs=[vm, vm, vm],
        out_specs=(vm, vm),
        scratch_shapes=[
            pltpu.VMEM((rows, wr, wc), BF16),
            pltpu.VMEM((rows, kc, wc), BF16),
            pltpu.VMEM((cols, 2 * wr, wc // 2), BF16),
            pltpu.VMEM((2 * wr, wc // 2), BF16),
            pltpu.VMEM((wc, wr), BF16),
            pltpu.VMEM((SIDE, SIDE, kb, wr), BF16),
            pltpu.VMEM((2, SIDE, kb, wr // 2), F32),
            pltpu.VMEM((2, SIDE, kb, wr // 2), BF16),
            pltpu.VMEM((2, SIDE - 1, SIDE, kb, wr // 2), BF16),
            pltpu.VMEM((2, SIDE - 1, kb, wr // 2), BF16),
            *pair_of(2, HOPS, CUTS), *pair_of(2, FAR), *pair_of(2, HOPS, CUTS), *pair_of(2, FAR),
            *pair_of(2),
            *pair_of(2), dma, dma, dma((2, NEAR, CUTS, 2)), dma((2, CUTS)), dma((CUTS, 2)),
            *pair_of(2, SIDE - 1), *pair_of(2, SIDE, SIDE - 1), *pair_of(2, SIDE - 1), *pair_of(2, SIDE - 1),
        ],
        compiler_params=pltpu.CompilerParams(
            collective_id=0, has_side_effects=True, vmem_limit_bytes=52 * 2**20
        ),
    )(factor, coupling.T, member.astype(F32)[None, :])
    return gram, child


def solution(mesh):
    return jax.shard_map(
        body,
        mesh=mesh,
        in_specs=(P("row", "col"), P(), P("col", "row")),
        out_specs=(P("row", "col"), P("col", "row")),
        check_vma=False,
    )
```

time: 111 us -> 107 us (0.964)
  the two profiles are of different devices: /device:TPU:1 before, /device:TPU:4 now
where the time goes in v3:
time: 107 us
  Pallas kernels  102 us (95%)
  local copies, waits for them, and re-layouts  3.86 us (4%)
    pallas_call x1, Pallas kernels, body(): pl.pallas_call(kernel, out_shape=(jax.ShapeDtypeStruct((wr, wc), F32), ja...  102 us
    unnamed x8, local copies, waits for them, and re-layouts  3.86 us

profile of v3, /device:TPU:4, one launch (start us, length us, event | category | flops | bytes accessed | tf_op | source)
XLA Modules:
  0.0 106.7 jit_solution(13947867960095153551)
XLA Ops:
  0.6 0.0 copy-start.2
  0.7 0.6 copy-done.2
  1.3 0.1 compare_reduce_fusion
  1.4 0.0 copy-start
  1.4 0.9 copy-done
  2.3 0.0 copy-start.1
  2.3 0.8 copy-done.1
  3.2 102.1 %shard_map.50 = (f32[256,512]{1,0:T(8,128)S(1)}, f32[128,256]{1,0:T(8,128)S(1)}) custom-call(bf16[256,512]{1,0:T(8,128)(2,1)S(1)} %copy-done, bf16[64,512]{1,0:T(8,128)(2,1)S(1)} %bitcast.2, f32[1,256]{1,0:T(1,128)S(1)} %bitcast.3), custom_call_target="tpu_custom_call" | custom-call | tf_op jit(solution)/shard_map/pallas_call | solution.py:530
  105.3 0.8 copy.7
  106.0 0.7 copy.8
  (2 shorter events, 0.0 us)
Async XLA Ops:
  0.6 0.7 copy-start.2
  1.4 0.9 copy-start
  2.3 0.8 copy-start.1

commit v4 on v3

--- a/solution.py
+++ b/solution.py
@@ -14,7 +14,7 @@
 FAR = N // 2
 CUTS = 2
 HOPS = FAR
-NEAR = 4
+NEAR = (6, 4)
 MIRRORED = 4
 EARLY = 5
 
@@ -146,7 +146,7 @@
         return both(core == k, lax.rem(m + FAR * k, N) == 0)
 
     def mirrors(m, plane):
-        return both(m >= plane, gap(m, plane) > NEAR)
+        return both(m - plane > NEAR[1], N - (m - plane) > NEAR[0])
 
     def leg2():
         return copy(stage, tp.at[z], leg2_send, leg2_recv, 2 * turn + core, col)
@@ -247,7 +247,7 @@
                 action(second(k, e, d, m))
 
     def starts_at(m):
-        return jnp.where(comes_at(m) <= NEAR, comes_at(m) + 1, MIRRORED)
+        return jnp.where(mirrors(m, z), MIRRORED, comes_at(m) + 1)
 
     def spread(s):
         @pl.when(both(mine >= z, starts_at(mine) == s))
@@ -298,7 +298,7 @@
                     def _():
                         to_pair(direction, s, h, m).start()
 
-                    @pl.when(both(col == z, m >= z, s <= NEAR))
+                    @pl.when(both(col == z, m >= z, s <= NEAR[direction]))
                     def _():
                         src = panel.at[slot_of(m), rows_of(h)]
                         hands(h, m, src, lambda k: hand_send.at[direction, s - 1, h, k])
@@ -307,7 +307,7 @@
         for direction in range(2):
             m = origin(direction, s)
 
-            @pl.when(s < FAR + 1 - direction)
+            @pl.when(both(s >= 1, s < FAR + 1 - direction))
             def _():
                 u_hop(direction, s, m, False).wait_recv()
 
@@ -319,7 +319,7 @@
 
     def ring_step(s, carry):
         passes(s)
-        u_passes(s)
+        u_passes(s - 1)
         spread(s)
         relay(s)
         return carry
@@ -367,6 +367,7 @@
         right = panel[pl.ds(2 * m, 2)].reshape(2 * wr, wc)
         g_ref[...] += lax.dot_general(left, right, (((0,), (0,)), ((), ())), preferred_element_type=F32)
 
+    u_passes(HOPS)
     with jax.named_scope("pairs"):
         spreads(True)
         for k in range(2):
@@ -484,13 +485,13 @@
                     for direction in range(2):
                         m = origin(direction, s)
 
-                        @pl.when(both(travels(m, direction, s, h), m >= z))
+                        @pl.when(both(travels(m, direction, s, h), m >= z, s <= NEAR[direction]))
                         def _():
                             handed(h, m, lambda k: hand_send.at[direction, s - 1, h, k])
 
                 return carry
 
-            lax.fori_loop(1, NEAR + 1, handed_on, 0)
+            lax.fori_loop(1, max(NEAR) + 1, handed_on, 0)
 
     with jax.named_scope("reduce1"):
         for k in range(2):
@@ -548,7 +549,7 @@
             pltpu.VMEM((2, SIDE - 1, kb, wr // 2), BF16),
             *pair_of(2, HOPS, CUTS), *pair_of(2, FAR), *pair_of(2, HOPS, CUTS), *pair_of(2, FAR),
             *pair_of(2),
-            *pair_of(2), dma, dma, dma((2, NEAR, CUTS, 2)), dma((2, CUTS)), dma((CUTS, 2)),
+            *pair_of(2), dma, dma, dma((2, max(NEAR), CUTS, 2)), dma((2, CUTS)), dma((CUTS, 2)),
             *pair_of(2, SIDE - 1), *pair_of(2, SIDE, SIDE - 1), *pair_of(2, SIDE - 1), *pair_of(2, SIDE - 1),
         ],
         compiler_params=pltpu.CompilerParams(

time: 107 us -> 103 us (0.963)
  the two profiles are of different devices: /device:TPU:4 before, /device:TPU:1 now
where the time goes in v4:
time: 103 us
  Pallas kernels  98.4 us (96%)
  local copies, waits for them, and re-layouts  3.86 us (4%)
    pallas_call x1, Pallas kernels, body(): pl.pallas_call(kernel, out_shape=(jax.ShapeDtypeStruct((wr, wc), F32), ja...  98.4 us
    unnamed x8, local copies, waits for them, and re-layouts  3.86 us

profile of v4, /device:TPU:1, one launch (start us, length us, event | category | flops | bytes accessed | tf_op | source)
XLA Modules:
  0.0 103.0 jit_solution(8035941762877272705)
XLA Ops:
  0.6 0.0 copy-start.2
  0.7 0.6 copy-done.2
  1.3 0.1 compare_reduce_fusion
  1.4 0.0 copy-start
  1.4 0.9 copy-done
  2.3 0.0 copy-start.1
  2.3 0.8 copy-done.1
  3.2 98.4 %shard_map.50 = (f32[256,512]{1,0:T(8,128)S(1)}, f32[128,256]{1,0:T(8,128)S(1)}) custom-call(bf16[256,512]{1,0:T(8,128)(2,1)S(1)} %copy-done, bf16[64,512]{1,0:T(8,128)(2,1)S(1)} %bitcast.2, f32[1,256]{1,0:T(1,128)S(1)} %bitcast.3), custom_call_target="tpu_custom_call" | custom-call | tf_op jit(solution)/shard_map/pallas_call | solution.py:531
  101.6 0.8 copy.7
  102.4 0.7 copy.8
  (2 shorter events, 0.0 us)
Async XLA Ops:
  0.6 0.7 copy-start.2
  1.4 0.9 copy-start
  2.3 0.8 copy-start.1

commit v5 on v4

--- a/solution.py
+++ b/solution.py
@@ -12,11 +12,12 @@
 SIDE = 4
 N = SIDE * SIDE
 FAR = N // 2
+SHIFT = 9
 CUTS = 2
 HOPS = FAR
 NEAR = (6, 4)
 MIRRORED = 4
-EARLY = 5
+EARLY = 4
 
 
 def both(*conditions):
@@ -76,7 +77,7 @@
     def greet(r, c):
         pl.semaphore_signal(barrier, inc=1, device_id=(r, c), device_id_type=MESH)
 
-    turn = lax.rem(col + 2 * N - z - FAR * core, N)
+    turn = lax.rem(col + 2 * N - z - SHIFT * core, N)
     for r in (up, down, partner):
         greet(r, col)
     for d in range(1, N):
@@ -137,13 +138,13 @@
     my_rows = pl.ds(pl.multiple_of(core * wr, wr), wr)
 
     def leg1(k, dst):
-        to = lax.rem(z + col + FAR * k, N)
+        to = lax.rem(z + col + SHIFT * k, N)
         return copy(
             w_ref.at[:, pl.ds(k * half, half)], dst, leg1_send.at[k], leg1_recv.at[core], 2 * z + k, to
         )
 
     def stays(k, m):
-        return both(core == k, lax.rem(m + FAR * k, N) == 0)
+        return both(core == k, lax.rem(m + SHIFT * k, N) == 0)
 
     def mirrors(m, plane):
         return both(m - plane > NEAR[1], N - (m - plane) > NEAR[0])
@@ -170,7 +171,7 @@
         return copy(
             src.at[:, pl.ds(k * half, half)],
             tp.at[m, pl.ds(pl.multiple_of(core * wr + h * chunk, chunk), chunk)],
-            sem, hand_recv.at[core, h], 2 * z + k, lax.rem(m + z + FAR * k, N),
+            sem, hand_recv.at[core, h], 2 * z + k, lax.rem(m + z + SHIFT * k, N),
         )
 
     def hands(h, m, src, sem_of):
@@ -211,7 +212,7 @@
         return x * SIDE + lax.rem(y + d, SIDE)
 
     def row_of(c):
-        return lax.rem(c + 2 * N - z - FAR * core, N)
+        return lax.rem(c + 2 * N - z - SHIFT * core, N)
 
     def least(k, c):
         return c // SIDE * SIDE if k == 0 else lax.rem(c, SIDE)
@@ -367,7 +368,6 @@
         right = panel[pl.ds(2 * m, 2)].reshape(2 * wr, wc)
         g_ref[...] += lax.dot_general(left, right, (((0,), (0,)), ((), ())), preferred_element_type=F32)
 
-    u_passes(HOPS)
     with jax.named_scope("pairs"):
         spreads(True)
         for k in range(2):
@@ -387,6 +387,7 @@
     with jax.named_scope("gram"):
         add_blocks(True)
 
+    u_passes(HOPS)
     with jax.named_scope("last"):
         spreads(False)
         lax.fori_loop(EARLY + 1, HOPS + 1, pairs, 0)

time: 103 us -> 103 us (level)
  the two profiles are of different devices: /device:TPU:1 before, /device:TPU:96 now
where the time goes in v5:
time: 103 us; the launch traced here: 102 us
  Pallas kernels  97.9 us (95%)
  local copies, waits for them, and re-layouts  3.86 us (4%)
    pallas_call x1, Pallas kernels, body(): pl.pallas_call(kernel, out_shape=(jax.ShapeDtypeStruct((wr, wc), F32), ja...  97.9 us
    unnamed x8, local copies, waits for them, and re-layouts  3.86 us

profile of v5, /device:TPU:96, one launch (start us, length us, event | category | flops | bytes accessed | tf_op | source)
XLA Modules:
  0.0 102.5 jit_solution(5662726811894021575)
XLA Ops:
  0.6 0.0 copy-start.2
  0.7 0.6 copy-done.2
  1.3 0.1 compare_reduce_fusion
  1.4 0.0 copy-start
  1.4 0.9 copy-done
  2.3 0.0 copy-start.1
  2.3 0.8 copy-done.1
  3.2 97.9 %shard_map.50 = (f32[256,512]{1,0:T(8,128)S(1)}, f32[128,256]{1,0:T(8,128)S(1)}) custom-call(bf16[256,512]{1,0:T(8,128)(2,1)S(1)} %copy-done, bf16[64,512]{1,0:T(8,128)(2,1)S(1)} %bitcast.2, f32[1,256]{1,0:T(1,128)S(1)} %bitcast.3), custom_call_target="tpu_custom_call" | custom-call | tf_op jit(solution)/shard_map/pallas_call | solution.py:532
  101.0 0.8 copy.7
  101.8 0.7 copy.8
  (2 shorter events, 0.0 us)
Async XLA Ops:
  0.6 0.7 copy-start.2
  1.4 0.9 copy-start
  2.3 0.8 copy-start.1

commit v6 on v5

--- a/solution.py
+++ b/solution.py
@@ -16,7 +16,7 @@
 CUTS = 2
 HOPS = FAR
 NEAR = (6, 4)
-MIRRORED = 4
+MIRRORED = 5
 EARLY = 4
 
 

time: 103 us -> 102 us (level)
  the two profiles are of different devices: /device:TPU:96 before, /device:TPU:6 now
where the time goes in v6:
time: 102 us
  Pallas kernels  97.2 us (95%)
  local copies, waits for them, and re-layouts  3.86 us (4%)
    pallas_call x1, Pallas kernels, body(): pl.pallas_call(kernel, out_shape=(jax.ShapeDtypeStruct((wr, wc), F32), ja...  97.2 us
    unnamed x8, local copies, waits for them, and re-layouts  3.86 us

profile of v6, /device:TPU:6, one launch (start us, length us, event | category | flops | bytes accessed | tf_op | source)
XLA Modules:
  0.0 101.9 jit_solution(534166669689805927)
XLA Ops:
  0.6 0.0 copy-start.2
  0.7 0.6 copy-done.2
  1.3 0.1 compare_reduce_fusion
  1.4 0.0 copy-start
  1.4 0.9 copy-done
  2.3 0.0 copy-start.1
  2.3 0.8 copy-done.1
  3.2 97.2 %shard_map.50 = (f32[256,512]{1,0:T(8,128)S(1)}, f32[128,256]{1,0:T(8,128)S(1)}) custom-call(bf16[256,512]{1,0:T(8,128)(2,1)S(1)} %copy-done, bf16[64,512]{1,0:T(8,128)(2,1)S(1)} %bitcast.2, f32[1,256]{1,0:T(1,128)S(1)} %bitcast.3), custom_call_target="tpu_custom_call" | custom-call | tf_op jit(solution)/shard_map/pallas_call | solution.py:532
  100.4 0.8 copy.7
  101.2 0.7 copy.8
  (2 shorter events, 0.0 us)
Async XLA Ops:
  0.6 0.7 copy-start.2
  1.4 0.9 copy-start
  2.3 0.8 copy-start.1
